TPU v7x, 32 devices: a whole 2x2x4 slice. The times are simulated.
32 devices in a mesh: space: 8 (over y, x, core), level: 4 (over z).
Axes of the slice: x: 2, y: 2, z: 4, core: 2. Of those that a mesh axis runs over, the one named last changes fastest.
Arguments:
- levels_in: bfloat16 [12, 48, 384, 512], P('level', 'space'), may hold values from -6 to 6
- kv_gain: float32 [512], replicated, may hold values from 0.25 to 1.75
- level_embed: float32 [12, 512], P('level'), may hold values from -3 to 3
- latent_queries: float32 [3, 512], replicated, may hold values from -6 to 6
- q_weight: bfloat16 [512, 512], replicated, may hold values from -0.25 to 0.25
- k_weight: bfloat16 [512, 512], replicated, may hold values from -0.25 to 0.25
- v_weight: bfloat16 [512, 512], replicated, may hold values from -0.25 to 0.25
- out_weight: bfloat16 [512, 512], replicated, may hold values from -0.25 to 0.25
- perc_scale: float32 [8], replicated, may hold values from 4 to 24
- attn_gain: float32 [512], replicated, may hold values from 0.25 to 1.75
- qkv_weight: bfloat16 [512, 1536], replicated, may hold values from -0.25 to 0.25
- swin_scale: float32 [8], replicated, may hold values from 4 to 24
- proj_weight: bfloat16 [512, 512], replicated, may hold values from -0.25 to 0.25
- mlp_gain: float32 [512], replicated, may hold values from 0.25 to 1.75
- up_weight: bfloat16 [512, 2048], replicated, may hold values from -0.25 to 0.25
- down_weight: bfloat16 [2048, 512], replicated, may hold values from -0.125 to 0.125
Outputs:
- latent_out: bfloat16 [3, 48, 384, 512], P(None, 'space', 'level')
All inputs are finite; a program needn't handle non-finite values.
Results may differ from a plain program's by a relative error of at most 0.017.
Values may be sent and summed in bfloat16 or wider, within the bound.
A program may use at most 128 MiB of HBM per device.

v0:
```python
import functools

import jax
import jax.numpy as jnp
from jax import lax
from jax.experimental import pallas as pl
from jax.experimental.pallas import tpu as pltpu
from jax.sharding import PartitionSpec as P

WR = 6
WC = 12
SR = 3
SC = 6
LANES = 128
STEP = 2 * WC
EDGE = 8
BF = jnp.bfloat16
F32 = jnp.float32
MESH = pl.DeviceIdType.MESH


def dot(a, b):
    return jnp.dot(a, b, preferred_element_type=F32)


def dot_t(a, b):
    return lax.dot_general(a, b, (((1,), (1,)), ((), ())), preferred_element_type=F32)


def iota(shape, axis):
    return lax.broadcasted_iota(jnp.int32, shape, axis)


def layer_norm(values, gain):
    center = values - jnp.mean(values, -1, keepdims=True)
    spread = jnp.mean(center * center, -1, keepdims=True)
    return center * lax.rsqrt(spread + 1e-05) * gain


def kernel(
    levels_hbm,
    kv_gain,
    embed,
    lq,
    q_hbm,
    k_hbm,
    v_hbm,
    out_hbm,
    perc,
    attn_gain,
    qkv_hbm,
    swin,
    proj_hbm,
    mlp_gain,
    up_hbm,
    down_hbm,
    p_hbm,
    q_w,
    k_w,
    v_w,
    out_w,
    qkv_w,
    proj_w,
    up_w,
    down_w,
    xa,
    xb,
    mine,
    from_left,
    from_right,
    total,
    head,
    tail,
    ahead,
    own,
    back,
    q_mat,
    ones,
    spread,
    den_spread,
    ones_t,
    padded,
    w_sem,
    xa_sem,
    xb_sem,
    z_send,
    left_recv,
    right_recv,
    head_send,
    head_recv,
    own_sem,
    back_send,
    back_recv,
    edge_send,
    edge_recv,
):
    levels, rows, all_cols, width = levels_hbm.shape
    latents = lq.shape[0]
    heads = perc.shape[0]
    head_dim = width // heads
    n = lax.axis_size("level")
    spaces = lax.axis_size("space")
    me = lax.axis_index("level")
    place = lax.axis_index("space")
    cols = all_cols // n
    chunks = cols // STEP
    tokens = rows * STEP
    half = SR * STEP
    side = latents * half
    packed_rows = latents * tokens + 16

    up_level = lax.rem(me + 1, n)
    down_level = lax.rem(me + n - 1, n)
    up_space = lax.rem(place + 1, spaces)
    down_space = lax.rem(place + spaces - 1, spaces)

    barrier = pltpu.get_barrier_semaphore()
    for target in (
        {"level": up_level},
        {"level": down_level},
        {"space": up_space},
        {"space": down_space},
        {"space": up_space, "level": up_level},
        {"space": down_space, "level": down_level},
    ):
        pl.semaphore_signal(barrier, inc=1, device_id=target, device_id_type=MESH)

    def dest_of(j):
        return jnp.where(2 * me < n, n - 1 - j, j)

    def chunk_of(i):
        return lax.rem(i + chunks - 1, chunks)

    def weight_copies():
        pairs = (
            (q_hbm, q_w),
            (k_hbm, k_w),
            (v_hbm, v_w),
            (out_hbm, out_w),
            (qkv_hbm, qkv_w),
            (proj_hbm, proj_w),
            (up_hbm, up_w),
            (down_hbm, down_w),
        )
        return [pltpu.make_async_copy(a, b, w_sem.at[i]) for i, (a, b) in enumerate(pairs)]

    def x_copies(i, j):
        slot = lax.rem(i, 2) * n + j
        start = pl.multiple_of(dest_of(j) * cols + chunk_of(i) * STEP, EDGE)
        rest = pl.multiple_of(lax.rem(start + STEP, all_cols), EDGE)
        return (
            pltpu.make_async_copy(
                levels_hbm.at[:, :, pl.ds(start, STEP)], xa.at[slot], xa_sem.at[slot]
            ),
            pltpu.make_async_copy(
                levels_hbm.at[:, :, pl.ds(rest, EDGE)], xb.at[slot], xb_sem.at[slot]
            ),
        )

    def start_x(i):
        def body(j, carry):
            for copy in x_copies(i, j):
                copy.start()
            return carry

        lax.fori_loop(0, n, body, 0)

    def send_right(d, i):
        return pltpu.make_async_remote_copy(
            src_ref=mine.at[d, i],
            dst_ref=from_left.at[d, i],
            send_sem=z_send.at[d, i],
            recv_sem=left_recv.at[d, i],
            device_id={"level": up_level},
            device_id_type=MESH,
        )

    def send_left(d, i):
        return pltpu.make_async_remote_copy(
            src_ref=mine.at[d, i],
            dst_ref=from_right.at[d, i],
            send_sem=z_send.at[d, i],
            recv_sem=right_recv.at[d, i],
            device_id={"level": down_level},
            device_id_type=MESH,
        )

    def send_head(i):
        return pltpu.make_async_remote_copy(
            src_ref=head.at[i],
            dst_ref=ahead.at[i],
            send_sem=head_send.at[i],
            recv_sem=head_recv.at[i],
            device_id={"space": down_space},
            device_id_type=MESH,
        )

    def column_of(i):
        return pl.multiple_of(EDGE + chunk_of(i) * STEP, EDGE)

    def send_back(i):
        return pltpu.make_async_remote_copy(
            src_ref=back.at[i],
            dst_ref=p_hbm.at[:, pl.ds(0, SR), pl.ds(column_of(i), STEP)],
            send_sem=back_send.at[i],
            recv_sem=back_recv.at[i],
            device_id={"space": up_space},
            device_id_type=MESH,
        )

    def keep_own(i):
        return pltpu.make_async_copy(
            own.at[i],
            p_hbm.at[:, pl.ds(SR, SR), pl.ds(column_of(i), STEP)],
            own_sem.at[i],
        )

    def edge_copies():
        cut = pl.ds(STEP - EDGE, EDGE)
        return (
            pltpu.make_async_remote_copy(
                src_ref=own.at[0, :, :, cut],
                dst_ref=p_hbm.at[:, pl.ds(SR, SR), pl.ds(0, EDGE)],
                send_sem=edge_send.at[0],
                recv_sem=edge_recv.at[0],
                device_id={"level": up_level},
                device_id_type=MESH,
            ),
            pltpu.make_async_remote_copy(
                src_ref=back.at[0, :, :, cut],
                dst_ref=p_hbm.at[:, pl.ds(0, SR), pl.ds(0, EDGE)],
                send_sem=edge_send.at[1],
                recv_sem=edge_recv.at[1],
                device_id={"space": up_space, "level": up_level},
                device_id_type=MESH,
            ),
        )

    weights = weight_copies()
    weights[0].start()
    weights[1].start()
    weights[2].start()
    start_x(0)

    lane = iota((latents, width), 1) // head_dim
    ones[...] = (
        (iota((width, LANES), 0) // head_dim == lax.rem(iota((width, LANES), 1), heads))
        & (iota((width, LANES), 1) < latents * heads)
    ).astype(F32).astype(BF)
    for a in range(latents):
        spread[:, a * width : (a + 1) * width] = (
            iota((LANES, width), 0) == iota((LANES, width), 1) // head_dim + a * heads
        ).astype(F32).astype(BF)
    for t in range(2):
        den_spread[t] = (
            iota((16, width), 0) - t * heads == iota((16, width), 1) // head_dim
        ).astype(F32).astype(BF)
    ones_t[...] = (iota((16, width), 0) == iota((16, width), 1) // head_dim).astype(F32).astype(BF)

    padded[...] = jnp.zeros_like(padded)
    padded[0:latents, :] = lq[...]
    weights[0].wait()
    queries = dot(padded[...].astype(BF), q_w[...])[:8]
    squares = queries * queries
    lane8 = iota((8, width), 1) // head_dim
    factor = jnp.zeros((8, width), F32)
    for h in range(heads):
        mean = jnp.sum(jnp.where(lane8 == h, squares, 0.0), -1, keepdims=True) / head_dim
        scale = lax.rsqrt(mean + 1e-06) * (perc[h] / head_dim)
        factor = jnp.where(lane8 == h, scale, factor)
    unit = queries * factor
    own_head = iota((heads, width), 0) == iota((heads, width), 1) // head_dim
    parts = [jnp.where(own_head, unit[a : a + 1], 0.0) for a in range(latents)]
    parts.append(jnp.zeros((LANES - latents * heads, width), F32))
    q_rows = jnp.concatenate(parts, 0)
    q_high = q_rows.astype(BF)
    q_mat[:LANES, :] = q_high
    q_mat[LANES:, :] = (q_rows - q_high.astype(F32)).astype(BF)

    weights[1].wait()
    weights[2].wait()
    for copy in weights[3:]:
        copy.start()
    pl.semaphore_wait(barrier, 6)

    def partial(i, j):
        slot = lax.rem(i, 2) * n + j
        d = dest_of(j)
        for copy in x_copies(i, j):
            copy.wait()
        normed = []
        for l in range(levels):
            x = jnp.concatenate([xa[slot, l].astype(F32), xb[slot, l].astype(F32)], 1)
            x = x[:, SC : SC + STEP].reshape(tokens, width)
            x = layer_norm(x, kv_gain[...]) + embed[l : l + 1, :]
            normed.append(x.astype(BF))
        normed = jnp.concatenate(normed, 0)
        keys = dot(normed, k_w[...]).astype(BF)
        values = dot(normed, v_w[...]).astype(BF).astype(F32)
        keys32 = keys.astype(F32)
        squares = dot((keys32 * keys32).astype(BF), ones[...])
        raw = dot_t(keys, q_mat[...])
        raw = raw[:, :LANES] + raw[:, LANES:]
        weights = jnp.exp(raw * lax.rsqrt(squares * (1.0 / head_dim) + 1e-06))
        denom = weights[:tokens]
        for l in range(1, levels):
            denom = denom + weights[l * tokens : (l + 1) * tokens]
        low = weights.astype(BF)
        for a in range(latents):
            wide = dot(low, spread[:, a * width : (a + 1) * width]) * values
            numer = wide[:tokens]
            for l in range(1, levels):
                numer = numer + wide[l * tokens : (l + 1) * tokens]
            mine[d, i, a * tokens : (a + 1) * tokens, :] = numer.astype(BF)
        pad = 2 * LANES - tokens
        turned = jnp.concatenate([denom, jnp.ones((pad, LANES), F32)], 0).T
        halves = []
        for t in range(2):
            cut = slice(t * LANES, (t + 1) * LANES)
            row = [turned[a * 8 : a * 8 + 8, cut] for a in range(latents)]
            row.append(jnp.ones((8, width - latents * LANES), F32))
            halves.append(jnp.concatenate(row, 1))
        mine[d, i, latents * tokens :, :] = jnp.concatenate(halves, 0).astype(BF)

        @pl.when((me == 0) & (d != me))
        def _():
            send_right(d, i).start()

        @pl.when((me == n - 1) & (d != me))
        def _():
            send_left(d, i).start()

    def forward(i, j):
        d = dest_of(j)

        @pl.when((d > me) & (me > 0))
        def _():
            send_right(d, i).wait_recv()
            mine[d, i] = (mine[d, i].astype(F32) + from_left[d, i].astype(F32)).astype(BF)
            send_right(d, i).start()

        @pl.when((d < me) & (me < n - 1))
        def _():
            send_left(d, i).wait_recv()
            mine[d, i] = (mine[d, i].astype(F32) + from_right[d, i].astype(F32)).astype(BF)
            send_left(d, i).start()

    def latent(i):
        total[...] = mine[me, i].astype(F32)

        @pl.when(me > 0)
        def _():
            send_right(me, i).wait_recv()
            total[...] += from_left[me, i].astype(F32)

        @pl.when(me < n - 1)
        def _():
            send_left(me, i).wait_recv()
            total[...] += from_right[me, i].astype(F32)

        turned = total[latents * tokens :, :].T.astype(BF)
        for a in range(latents):
            block = turned[a * LANES : (a + 1) * LANES]
            denom = jnp.concatenate(
                [dot(block, den_spread[0]), dot(block, den_spread[1])[: tokens - LANES]], 0
            )
            pooled = (total[a * tokens : (a + 1) * tokens, :] / denom).astype(BF)
            value = lq[a : a + 1, :] + dot(pooled, out_w[...])
            head[i, a] = value[:half].astype(BF)
            tail[a] = value[half:].astype(BF)
        send_head(i).start()

    scale_row = jnp.zeros((1, LANES), F32)
    for h in range(heads):
        scale_row = jnp.where(iota((1, LANES), 1) == h, swin[h] / head_dim, scale_row)

    def layer(i):
        send_head(i).wait_recv()
        block = jnp.concatenate(
            [
                tail[...].astype(F32).reshape(side, width),
                ahead[i].astype(F32).reshape(side, width),
            ],
            0,
        )
        normed = layer_norm(block, attn_gain[...]).astype(BF)
        packed = dot(normed, qkv_w[...]).astype(BF)
        q = packed[:, :width]
        k = packed[:, width : 2 * width]
        v = packed[:, 2 * width :]
        q32 = q.astype(F32)
        k32 = k.astype(F32)
        q_norm = dot((q32 * q32).astype(BF), ones[...])
        q_norm = lax.rsqrt(q_norm * (1.0 / head_dim) + 1e-06) * scale_row
        k_norm = dot_t(ones_t[...], (k32 * k32).astype(BF))
        k_norm = lax.rsqrt(k_norm * (1.0 / head_dim) + 1e-06)
        row = iota((2 * side, 2 * side), 0)
        col = iota((2 * side, 2 * side), 1)
        window = lax.rem(row, STEP) // WC == lax.rem(col, STEP) // WC
        region = (row >= side) == (col >= side)
        mask = jnp.where(window & (region | (place < spaces - 1)), 1.0, 0.0)
        mixed = []
        for h in range(heads):
            cut = slice(h * head_dim, (h + 1) * head_dim)
            scores = dot_t(q[:, cut], k[:, cut])
            scores = scores * q_norm[:, h : h + 1] * k_norm[h : h + 1, :]
            weights = jnp.exp(scores) * mask
            norm = jnp.sum(weights, -1, keepdims=True)
            mixed.append(dot(weights.astype(BF), v[:, cut]) / norm)
        mixed = jnp.concatenate(mixed, 1).astype(BF)
        branch = dot(mixed, proj_w[...]).astype(BF)
        middle = block + branch.astype(F32)
        mlp_in = layer_norm(middle, mlp_gain[...]).astype(BF)
        hidden = jax.nn.gelu(dot(mlp_in, up_w[...])).astype(BF)
        final = middle + dot(hidden, down_w[...])
        own[i] = final[:side].reshape(latents, SR, STEP, width).astype(BF)
        back[i] = final[side:].reshape(latents, SR, STEP, width).astype(BF)
        keep_own(i).start()
        send_back(i).start()

        @pl.when(i == 0)
        def _():
            for copy in edge_copies():
                copy.start()

    def step(s, carry):
        t = s - 1

        @pl.when(t >= 1)
        def _():
            @pl.when(t == 1)
            def _():
                for copy in weights[3:]:
                    copy.wait()

            latent(t - 1)

        @pl.when(t + 2 < chunks)
        def _():
            start_x(t + 2)

        @pl.when(t + 1 < chunks)
        def _():
            def body(j, c):
                partial(t + 1, j)
                return c

            lax.fori_loop(0, n, body, 0)

        @pl.when(t >= 1)
        def _():
            layer(t - 1)

        @pl.when((t >= 0) & (t < chunks))
        def _():
            def body(j, c):
                forward(t, j)
                return c

            lax.fori_loop(0, n, body, 0)

        return carry

    lax.fori_loop(0, chunks + 2, step, 0)

    def drain(i, carry):
        def each(d, c):
            @pl.when(d != me)
            def _():
                send_right(d, i).wait_send()

            return c

        lax.fori_loop(0, n, each, 0)
        send_head(i).wait_send()
        keep_own(i).wait()
        send_back(i).wait()
        return carry

    lax.fori_loop(0, chunks, drain, 0)
    for copy in edge_copies():
        copy.wait()


def shards(
    levels_in,
    kv_gain,
    level_embed,
    latent_queries,
    q_weight,
    k_weight,
    v_weight,
    out_weight,
    perc_scale,
    attn_gain,
    qkv_weight,
    swin_scale,
    proj_weight,
    mlp_gain,
    up_weight,
    down_weight,
):
    levels, rows, all_cols, width = levels_in.shape
    latents = latent_queries.shape[0]
    heads = perc_scale.shape[0]
    mlp = up_weight.shape[1]
    n = lax.axis_size("level")
    cols = all_cols // n
    chunks = cols // STEP
    tokens = rows * STEP
    half = SR * STEP
    packed_rows = latents * tokens + 16
    assert rows == WR and heads == 8 and LANES < tokens <= 2 * LANES
    assert cols % STEP == 0 and n >= 2

    hbm = pl.BlockSpec(memory_space=pl.ANY)
    vmem = pl.BlockSpec(memory_space=pltpu.VMEM)
    smem = pl.BlockSpec(memory_space=pltpu.SMEM)
    sem = pltpu.SemaphoreType.DMA
    padded = pl.pallas_call(
        kernel,
        in_specs=[hbm, vmem, vmem, vmem, hbm, hbm, hbm, hbm, smem, vmem, hbm, smem, hbm, vmem]
        + [hbm, hbm],
        out_specs=hbm,
        out_shape=jax.ShapeDtypeStruct((latents, rows, cols + EDGE, width), BF),
        scratch_shapes=[
            pltpu.VMEM((width, width), BF),
            pltpu.VMEM((width, width), BF),
            pltpu.VMEM((width, width), BF),
            pltpu.VMEM((width, width), BF),
            pltpu.VMEM((width, 3 * width), BF),
            pltpu.VMEM((width, width), BF),
            pltpu.VMEM((width, mlp), BF),
            pltpu.VMEM((mlp, width), BF),
            pltpu.VMEM((2 * n, levels, rows, STEP, width), BF),
            pltpu.VMEM((2 * n, levels, rows, EDGE, width), BF),
            pltpu.VMEM((n, chunks, packed_rows, width), BF),
            pltpu.VMEM((n, chunks, packed_rows, width), BF),
            pltpu.VMEM((n, chunks, packed_rows, width), BF),
            pltpu.VMEM((packed_rows, width), F32),
            pltpu.VMEM((chunks, latents, half, width), BF),
            pltpu.VMEM((latents, half, width), BF),
            pltpu.VMEM((chunks, latents, half, width), BF),
            pltpu.VMEM((chunks, latents, SR, STEP, width), BF),
            pltpu.VMEM((chunks, latents, SR, STEP, width), BF),
            pltpu.VMEM((2 * LANES, width), BF),
            pltpu.VMEM((width, LANES), BF),
            pltpu.VMEM((LANES, latents * width), BF),
            pltpu.VMEM((2, 16, width), BF),
            pltpu.VMEM((16, width), BF),
            pltpu.VMEM((16, width), F32),
            sem((8,)),
            sem((2 * n,)),
            sem((2 * n,)),
            sem((n, chunks)),
            sem((n, chunks)),
            sem((n, chunks)),
            sem((chunks,)),
            sem((chunks,)),
            sem((chunks,)),
            sem((chunks,)),
            sem((chunks,)),
            sem((2,)),
            sem((2,)),
        ],
        compiler_params=pltpu.CompilerParams(
            collective_id=0, has_side_effects=True, vmem_limit_bytes=63 * 1024 * 1024
        ),
        name="whole",
    )(
        levels_in,
        kv_gain[None],
        level_embed,
        latent_queries,
        q_weight,
        k_weight,
        v_weight,
        out_weight,
        perc_scale,
        attn_gain[None],
        qkv_weight,
        swin_scale,
        proj_weight,
        mlp_gain[None],
        up_weight,
        down_weight,
    )
    return padded[:, :, EDGE - SC : EDGE - SC + cols]


def solution(mesh):
    placed = (P("level", "space", None, None), P(), P("level", None)) + (P(),) * 13
    return jax.shard_map(
        shards,
        mesh=mesh,
        in_specs=placed,
        out_specs=P(None, "space", "level", None),
        check_vma=False,
    )
```

profile of v0, /device:TPU:0, one launch (start us, length us, event | category | flops | bytes accessed | tf_op | source)
XLA Modules:
  0.0 160.3 jit_solution(8171006825817084772)
XLA Ops:
  0.0 156.8 %whole.1 = bf16[3,6,104,512]{3,2,1,0:T(8,128)(2,1)} custom-call(bf16[3,6,384,512]{3,2,1,0:T(8,128)(2,1)} %levels_hbm.1, f32[1,512]{1,0:T(1,128)} %bitcast.3, f32[3,512]{1,0:T(4,128)} %embed.1, f32[3,512]{1,0:T(4,128)} %lq.1, bf16[512,512]{1,0:T(8,128)(2,1)} %q_hbm.1, bf16[512,512]{1,0:T(8,128)(2,1)} %k_hbm.1, bf16[512,512]{1,0:T(8,128)(2,1)} %v_hbm.1, ...), custom_call_target="tpu_custom_call" | custom-call | tf_op jit(solution)/shard_map/whole/pallas_call | solution.py:520
  156.8 3.5 %slice.3 = bf16[3,6,96,512]{3,2,1,0:T(8,128)(2,1)} slice(bf16[3,6,104,512]{3,2,1,0:T(8,128)(2,1)} %whole.1), slice={[0:3], [0:6], [2:98], [0:512]} | slice | bytes 3538944 | tf_op jit(solution)/shard_map/slice | solution.py:588
where the time goes:
time: 163 us; the launch traced here: 160 us
  Pallas kernels  157 us (96%)
  local copies, waits for them, and re-layouts  3.45 us (2%)
    pallas_call x1, Pallas kernels, shards(): pl.pallas_call(kernel, in_specs=[hbm, vmem, vmem, vmem, hbm, hbm, hbm, hb...  157 us
    slice x1, local copies, waits for them, and re-layouts, shards(): return padded[:, :, EDGE - SC:EDGE - SC + cols]  3.45 us

commit v1 on v0

v1 whole, which is shorter than its diff:
```python
import functools

import jax
import jax.numpy as jnp
from jax import lax
from jax.experimental import pallas as pl
from jax.experimental.pallas import tpu as pltpu
from jax.sharding import PartitionSpec as P

WR = 6
WC = 12
SR = 3
SC = 6
LANES = 128
STEP = 2 * WC
EDGE = 8
LEAD = 2
BF = jnp.bfloat16
F32 = jnp.float32
MESH = pl.DeviceIdType.MESH


def dot(a, b):
    return jnp.dot(a, b, preferred_element_type=F32)


def dot_t(a, b):
    return lax.dot_general(a, b, (((1,), (1,)), ((), ())), preferred_element_type=F32)


def iota(shape, axis):
    return lax.broadcasted_iota(jnp.int32, shape, axis)


def layer_norm(values, gain):
    center = values - jnp.mean(values, -1, keepdims=True)
    spread = jnp.mean(center * center, -1, keepdims=True)
    return center * lax.rsqrt(spread + 1e-05) * gain


def kernel(
    levels_hbm,
    kv_gain,
    embed,
    lq,
    q_hbm,
    k_hbm,
    v_hbm,
    out_hbm,
    perc,
    attn_gain,
    qkv_hbm,
    swin,
    proj_hbm,
    mlp_gain,
    up_hbm,
    down_hbm,
    p_hbm,
    q_w,
    k_w,
    v_w,
    out_w,
    qkv_w,
    proj_w,
    up_w,
    down_w,
    xa,
    xb,
    mine,
    arrived,
    head,
    tail,
    ahead,
    own,
    back,
    q_mat,
    ones,
    spread,
    den_spread,
    ones_t,
    padded,
    mask,
    w_sem,
    xa_sem,
    xb_sem,
    z_send,
    z_recv,
    head_send,
    head_recv,
    own_sem,
    back_send,
    back_recv,
    edge_send,
    edge_recv,
):
    levels, rows, all_cols, width = levels_hbm.shape
    latents = lq.shape[0]
    heads = perc.shape[0]
    head_dim = width // heads
    n = lax.axis_size("level")
    spaces = lax.axis_size("space")
    me = lax.axis_index("level")
    place = lax.axis_index("space")
    cols = all_cols // n
    chunks = cols // STEP
    units = 2 * chunks
    tokens = SR * STEP
    side = latents * tokens
    raw_rows = levels * tokens
    lead = LEAD
    is_end = (me == 0) | (me == n - 1)

    up_level = lax.rem(me + 1, n)
    down_level = lax.rem(me + n - 1, n)
    up_space = lax.rem(place + 1, spaces)
    down_space = lax.rem(place + spaces - 1, spaces)

    barrier = pltpu.get_barrier_semaphore()
    for target in (
        {"level": up_level},
        {"level": down_level},
        {"space": up_space},
        {"space": down_space},
        {"space": up_space, "level": up_level},
        {"space": down_space, "level": down_level},
    ):
        pl.semaphore_signal(barrier, inc=1, device_id=target, device_id_type=MESH)

    def dest_of(j):
        return jnp.where(2 * me < n, n - 1 - j, j)

    def lead_of(d):
        near = is_end & (jnp.abs(d - me) == 1)
        return jnp.where((d == me) | near, 0, jnp.where(d == dest_of(0), lead, lead - 1))

    def chunk_of(i):
        return lax.rem(i + chunks - 1, chunks)

    def weight_copies():
        pairs = (
            (q_hbm, q_w),
            (k_hbm, k_w),
            (v_hbm, v_w),
            (out_hbm, out_w),
            (qkv_hbm, qkv_w),
            (proj_hbm, proj_w),
            (up_hbm, up_w),
            (down_hbm, down_w),
        )
        return [pltpu.make_async_copy(a, b, w_sem.at[i]) for i, (a, b) in enumerate(pairs)]

    def x_copies(d, u):
        band = pl.ds(lax.rem(u, 2) * SR, SR)
        start = pl.multiple_of(d * cols + chunk_of(lax.div(u, 2)) * STEP, EDGE)
        rest = pl.multiple_of(lax.rem(start + STEP, all_cols), EDGE)
        return (
            pltpu.make_async_copy(
                levels_hbm.at[:, band, pl.ds(start, STEP)], xa.at[d, u], xa_sem.at[d, u]
            ),
            pltpu.make_async_copy(
                levels_hbm.at[:, band, pl.ds(rest, EDGE)], xb.at[d, u], xb_sem.at[d, u]
            ),
        )

    def each_unit(first, last, act):
        def body(k, carry):
            d = dest_of(lax.rem(k, n))
            u = lax.div(k, n) - lead + lead_of(d)

            @pl.when((u >= 0) & (u < units))
            def _():
                act(d, u)

            return carry

        lax.fori_loop(first, last, body, 0)

    def start_x(d, u):
        for copy in x_copies(d, u):
            copy.start()

    def send(d, u, right, count):
        return pltpu.make_async_remote_copy(
            src_ref=mine.at[d, u, pl.ds(0, count)],
            dst_ref=arrived.at[0 if right else 1, d, u, pl.ds(0, count)],
            send_sem=z_send.at[d, u],
            recv_sem=z_recv.at[0 if right else 1, d, u],
            device_id={"level": up_level if right else down_level},
            device_id_type=MESH,
        )

    sum_rows = mine.shape[2]

    def send_head(i):
        return pltpu.make_async_remote_copy(
            src_ref=head.at[i],
            dst_ref=ahead.at[i],
            send_sem=head_send.at[i],
            recv_sem=head_recv.at[i],
            device_id={"space": down_space},
            device_id_type=MESH,
        )

    def column_of(i):
        return pl.multiple_of(EDGE + chunk_of(i) * STEP, EDGE)

    def send_back(i):
        return pltpu.make_async_remote_copy(
            src_ref=back.at[i],
            dst_ref=p_hbm.at[:, pl.ds(0, SR), pl.ds(column_of(i), STEP)],
            send_sem=back_send.at[i],
            recv_sem=back_recv.at[i],
            device_id={"space": up_space},
            device_id_type=MESH,
        )

    def keep_own(i):
        return pltpu.make_async_copy(
            own.at[i],
            p_hbm.at[:, pl.ds(SR, SR), pl.ds(column_of(i), STEP)],
            own_sem.at[i],
        )

    def edge_copies():
        cut = pl.ds(STEP - EDGE, EDGE)
        return (
            pltpu.make_async_remote_copy(
                src_ref=own.at[0, :, :, cut],
                dst_ref=p_hbm.at[:, pl.ds(SR, SR), pl.ds(0, EDGE)],
                send_sem=edge_send.at[0],
                recv_sem=edge_recv.at[0],
                device_id={"level": up_level},
                device_id_type=MESH,
            ),
            pltpu.make_async_remote_copy(
                src_ref=back.at[0, :, :, cut],
                dst_ref=p_hbm.at[:, pl.ds(0, SR), pl.ds(0, EDGE)],
                send_sem=edge_send.at[1],
                recv_sem=edge_recv.at[1],
                device_id={"space": up_space, "level": up_level},
                device_id_type=MESH,
            ),
        )

    def level_tokens(d, u):
        for copy in x_copies(d, u):
            copy.wait()
        normed = []
        for l in range(levels):
            x = jnp.concatenate([xa[d, u, l].astype(F32), xb[d, u, l].astype(F32)], 1)
            x = x[:, SC : SC + STEP].reshape(tokens, width)
            normed.append(layer_norm(x, kv_gain[...]) + embed[l : l + 1, :])
        return jnp.concatenate(normed, 0)

    total_steps = (units + lead) * n
    early = (lead + 1) * n
    weights = weight_copies()
    each_unit(0, early, start_x)
    for copy in weights[:3]:
        copy.start()
    pl.semaphore_wait(barrier, 6)

    def send_tokens(d, u):
        @pl.when(d != me)
        def _():
            mine[d, u, :raw_rows, :] = level_tokens(d, u).astype(BF)

            @pl.when(me == 0)
            def _():
                send(d, u, True, raw_rows).start()

            @pl.when(me == n - 1)
            def _():
                send(d, u, False, raw_rows).start()

    @pl.when(is_end)
    def _():
        each_unit(0, early, send_tokens)

    each_unit(early, total_steps, start_x)
    for copy in weights[3:]:
        copy.start()

    @pl.when(is_end)
    def _():
        each_unit(early, total_steps, send_tokens)

    ones[...] = (
        (iota((width, LANES), 0) // head_dim == lax.rem(iota((width, LANES), 1), heads))
        & (iota((width, LANES), 1) < latents * heads)
    ).astype(F32).astype(BF)
    for a in range(latents):
        spread[:, a * width : (a + 1) * width] = (
            iota((LANES, width), 0) == iota((LANES, width), 1) // head_dim + a * heads
        ).astype(F32).astype(BF)
    den_spread[...] = (iota((16, width), 0) == iota((16, width), 1) // head_dim).astype(F32).astype(BF)
    ones_t[...] = den_spread[...]

    padded[...] = jnp.zeros_like(padded)
    padded[0:latents, :] = lq[...]
    weights[0].wait()
    queries = dot(padded[...].astype(BF), q_w[...])[:8]
    squares = queries * queries
    lane8 = iota((8, width), 1) // head_dim
    factor = jnp.zeros((8, width), F32)
    for h in range(heads):
        mean = jnp.sum(jnp.where(lane8 == h, squares, 0.0), -1, keepdims=True) / head_dim
        scale = lax.rsqrt(mean + 1e-06) * (perc[h] / head_dim)
        factor = jnp.where(lane8 == h, scale, factor)
    unit = queries * factor
    own_head = iota((heads, width), 0) == iota((heads, width), 1) // head_dim
    parts = [jnp.where(own_head, unit[a : a + 1], 0.0) for a in range(latents)]
    parts.append(jnp.zeros((LANES - latents * heads, width), F32))
    q_rows = jnp.concatenate(parts, 0)
    q_high = q_rows.astype(BF)
    q_mat[:LANES, :] = q_high
    q_mat[LANES:, :] = (q_rows - q_high.astype(F32)).astype(BF)

    weights[1].wait()
    weights[2].wait()

    def partial(normed):
        keys = dot(normed, k_w[...]).astype(BF)
        values = dot(normed, v_w[...]).astype(BF).astype(F32)
        keys32 = keys.astype(F32)
        squares = dot((keys32 * keys32).astype(BF), ones[...])
        raw = dot_t(keys, q_mat[...])
        raw = raw[:, :LANES] + raw[:, LANES:]
        weights = jnp.exp(raw * lax.rsqrt(squares * (1.0 / head_dim) + 1e-06))
        denom = weights[:tokens]
        count = normed.shape[0] // tokens
        for l in range(1, count):
            denom = denom + weights[l * tokens : (l + 1) * tokens]
        low = weights.astype(BF)
        parts = []
        for a in range(latents):
            wide = dot(low, spread[:, a * width : (a + 1) * width]) * values
            numer = wide[:tokens]
            for l in range(1, count):
                numer = numer + wide[l * tokens : (l + 1) * tokens]
            parts.append(numer)
        turned = jnp.concatenate([denom, jnp.ones((LANES - tokens, LANES), F32)], 0).T
        row = [turned[a * 8 : a * 8 + 8, :] for a in range(latents)]
        row.append(jnp.ones((8, width - latents * LANES), F32))
        parts.append(jnp.concatenate(row, 1))
        return jnp.concatenate(parts, 0)

    def collect(d, u):
        left = (me > 0) & (d >= me)
        right = (me < n - 1) & (d <= me)
        tokens_left = left & (me == 1)
        tokens_right = right & (me == n - 2)

        @pl.when(tokens_left)
        def _():
            send(d, u, True, raw_rows).wait_recv()

        @pl.when(tokens_right)
        def _():
            send(d, u, False, raw_rows).wait_recv()

        @pl.when(tokens_left | tokens_right)
        def _():
            which = jnp.where(me == 1, 0, 1)
            more = arrived[which, d, u, :raw_rows, :].astype(F32)
            both = jnp.concatenate([level_tokens(d, u), more], 0).astype(BF)
            mine[d, u] = partial(both).astype(BF)

        @pl.when(jnp.logical_not(tokens_left | tokens_right))
        def _():
            mine[d, u] = partial(level_tokens(d, u).astype(BF)).astype(BF)

        @pl.when(left & (me > 1))
        def _():
            send(d, u, True, sum_rows).wait_recv()
            mine[d, u] = (mine[d, u].astype(F32) + arrived[0, d, u].astype(F32)).astype(BF)

        @pl.when(right & (me < n - 2))
        def _():
            send(d, u, False, sum_rows).wait_recv()
            mine[d, u] = (mine[d, u].astype(F32) + arrived[1, d, u].astype(F32)).astype(BF)

        @pl.when(d > me)
        def _():
            send(d, u, True, sum_rows).start()

        @pl.when(d < me)
        def _():
            send(d, u, False, sum_rows).start()

    def latent(u):
        total = mine[me, u].astype(F32)
        turned = jnp.concatenate([total[side:], jnp.zeros((8, width), F32)], 0).T.astype(BF)
        pooled = []
        query = []
        for a in range(latents):
            denom = dot(turned[a * LANES : (a + 1) * LANES], den_spread[...])[:tokens]
            pooled.append(total[a * tokens : (a + 1) * tokens] / denom)
            query.append(jnp.broadcast_to(lq[a : a + 1, :], (tokens, width)))
        pooled = jnp.concatenate(pooled, 0).astype(BF)
        value = (jnp.concatenate(query, 0) + dot(pooled, out_w[...])).astype(BF)
        i = lax.div(u, 2)

        @pl.when(lax.rem(u, 2) == 0)
        def _():
            head[i] = value
            send_head(i).start()

        @pl.when(lax.rem(u, 2) == 1)
        def _():
            tail[...] = value

    scale_row = jnp.zeros((1, LANES), F32)
    for h in range(heads):
        scale_row = jnp.where(iota((1, LANES), 1) == h, swin[h] / head_dim, scale_row)
    row = iota((2 * side, 2 * side), 0)
    col = iota((2 * side, 2 * side), 1)
    window = lax.rem(row, STEP) // WC == lax.rem(col, STEP) // WC
    region = (row >= side) == (col >= side)
    mask[...] = jnp.where(window & (region | (place < spaces - 1)), 1.0, 0.0)

    def layer(i):
        send_head(i).wait_recv()
        block = jnp.concatenate([tail[...].astype(F32), ahead[i].astype(F32)], 0)
        normed = layer_norm(block, attn_gain[...]).astype(BF)
        packed = dot(normed, qkv_w[...]).astype(BF)
        q = packed[:, :width]
        k = packed[:, width : 2 * width]
        v = packed[:, 2 * width :]
        q32 = q.astype(F32)
        k32 = k.astype(F32)
        q_norm = dot((q32 * q32).astype(BF), ones[...])
        q_norm = lax.rsqrt(q_norm * (1.0 / head_dim) + 1e-06) * scale_row
        k_norm = dot_t(ones_t[...], (k32 * k32).astype(BF))
        k_norm = lax.rsqrt(k_norm * (1.0 / head_dim) + 1e-06)
        mixed = []
        for h in range(heads):
            cut = slice(h * head_dim, (h + 1) * head_dim)
            scores = dot_t(q[:, cut], k[:, cut])
            scores = scores * q_norm[:, h : h + 1] * k_norm[h : h + 1, :]
            weights = jnp.exp(scores) * mask[...]
            norm = jnp.sum(weights, -1, keepdims=True)
            mixed.append(dot(weights.astype(BF), v[:, cut]) / norm)
        mixed = jnp.concatenate(mixed, 1).astype(BF)
        branch = dot(mixed, proj_w[...]).astype(BF)
        middle = block + branch.astype(F32)

        def feed(part):
            mlp_in = layer_norm(part, mlp_gain[...]).astype(BF)
            hidden = jax.nn.gelu(dot(mlp_in, up_w[...])).astype(BF)
            final = part + dot(hidden, down_w[...])
            return final.reshape(latents, SR, STEP, width).astype(BF)

        back[i] = feed(middle[side:])
        send_back(i).start()
        own[i] = feed(middle[:side])
        keep_own(i).start()

        @pl.when(i == 0)
        def _():
            for copy in edge_copies():
                copy.start()

    def step(v, carry):
        def body(k, c):
            d = dest_of(jnp.where(k == 0, 0, jnp.where(k == 1, n - 1, k - 1)))
            u = v - lead + lead_of(d)

            @pl.when((u >= 0) & (u < units) & ((d == me) | jnp.logical_not(is_end)))
            def _():
                collect(d, u)

            return c

        lax.fori_loop(0, n, body, 0)

        @pl.when(v == lead)
        def _():
            for copy in weights[3:]:
                copy.wait()

        @pl.when(v >= lead)
        def _():
            latent(v - lead)

            @pl.when(lax.rem(v - lead, 2) == 1)
            def _():
                layer(lax.div(v - lead, 2))

        return carry

    lax.fori_loop(0, units + lead, step, 0)

    def drain(d, u):
        @pl.when((d != me) & is_end)
        def _():
            send(d, u, True, raw_rows).wait_send()

        @pl.when((d != me) & jnp.logical_not(is_end))
        def _():
            send(d, u, True, sum_rows).wait_send()

    each_unit(0, total_steps, drain)

    def finish(i, carry):
        send_head(i).wait_send()
        keep_own(i).wait()
        send_back(i).wait()
        return carry

    lax.fori_loop(0, chunks, finish, 0)
    for copy in edge_copies():
        copy.wait()


def shards(
    levels_in,
    kv_gain,
    level_embed,
    latent_queries,
    q_weight,
    k_weight,
    v_weight,
    out_weight,
    perc_scale,
    attn_gain,
    qkv_weight,
    swin_scale,
    proj_weight,
    mlp_gain,
    up_weight,
    down_weight,
):
    levels, rows, all_cols, width = levels_in.shape
    latents = latent_queries.shape[0]
    heads = perc_scale.shape[0]
    mlp = up_weight.shape[1]
    n = lax.axis_size("level")
    cols = all_cols // n
    chunks = cols // STEP
    units = 2 * chunks
    tokens = SR * STEP
    side = latents * tokens
    sum_rows = side + 8
    assert rows == WR and heads == 8 and tokens <= LANES and latents * heads <= LANES
    assert cols % STEP == 0 and n >= 4 and levels * tokens <= sum_rows

    hbm = pl.BlockSpec(memory_space=pl.ANY)
    vmem = pl.BlockSpec(memory_space=pltpu.VMEM)
    smem = pl.BlockSpec(memory_space=pltpu.SMEM)
    sem = pltpu.SemaphoreType.DMA
    padded = pl.pallas_call(
        kernel,
        in_specs=[hbm, vmem, vmem, vmem, hbm, hbm, hbm, hbm, smem, vmem, hbm, smem, hbm, vmem]
        + [hbm, hbm],
        out_specs=hbm,
        out_shape=jax.ShapeDtypeStruct((latents, rows, cols + EDGE, width), BF),
        scratch_shapes=[
            pltpu.VMEM((width, width), BF),
            pltpu.VMEM((width, width), BF),
            pltpu.VMEM((width, width), BF),
            pltpu.VMEM((width, width), BF),
            pltpu.VMEM((width, 3 * width), BF),
            pltpu.VMEM((width, width), BF),
            pltpu.VMEM((width, mlp), BF),
            pltpu.VMEM((mlp, width), BF),
            pltpu.VMEM((n, units, levels, SR, STEP, width), BF),
            pltpu.VMEM((n, units, levels, SR, EDGE, width), BF),
            pltpu.VMEM((n, units, sum_rows, width), BF),
            pltpu.VMEM((2, n, units, sum_rows, width), BF),
            pltpu.VMEM((chunks, side, width), BF),
            pltpu.VMEM((side, width), BF),
            pltpu.VMEM((chunks, side, width), BF),
            pltpu.VMEM((chunks, latents, SR, STEP, width), BF),
            pltpu.VMEM((chunks, latents, SR, STEP, width), BF),
            pltpu.VMEM((2 * LANES, width), BF),
            pltpu.VMEM((width, LANES), BF),
            pltpu.VMEM((LANES, latents * width), BF),
            pltpu.VMEM((16, width), BF),
            pltpu.VMEM((16, width), BF),
            pltpu.VMEM((16, width), F32),
            pltpu.VMEM((2 * side, 2 * side), F32),
            sem((8,)),
            sem((n, units)),
            sem((n, units)),
            sem((n, units)),
            sem((2, n, units)),
            sem((chunks,)),
            sem((chunks,)),
            sem((chunks,)),
            sem((chunks,)),
            sem((chunks,)),
            sem((2,)),
            sem((2,)),
        ],
        compiler_params=pltpu.CompilerParams(
            collective_id=0, has_side_effects=True, vmem_limit_bytes=63 * 1024 * 1024
        ),
        name="whole",
    )(
        levels_in,
        kv_gain[None],
        level_embed,
        latent_queries,
        q_weight,
        k_weight,
        v_weight,
        out_weight,
        perc_scale,
        attn_gain[None],
        qkv_weight,
        swin_scale,
        proj_weight,
        mlp_gain[None],
        up_weight,
        down_weight,
    )
    return padded[:, :, EDGE - SC : EDGE - SC + cols]


def solution(mesh):
    placed = (P("level", "space", None, None), P(), P("level", None)) + (P(),) * 13
    return jax.shard_map(
        shards,
        mesh=mesh,
        in_specs=placed,
        out_specs=P(None, "space", "level", None),
        check_vma=False,
    )
```

time: 163 us -> 145 us (0.89); the launches traced: 160 us -> 145 us
  Pallas kernels: 157 us -> 141 us
    pallas_call x1, Pallas kernels: 157 us -> 141 us  [shards(): pl.pallas_call(kernel, in_specs=[hbm, vmem, vmem, vmem, hbm, hbm, hbm, hb...]
where the time goes in v1:
time: 145 us
  Pallas kernels  141 us (97%)
  local copies, waits for them, and re-layouts  3.45 us (2%)
    pallas_call x1, Pallas kernels, shards(): pl.pallas_call(kernel, in_specs=[hbm, vmem, vmem, vmem, hbm, hbm, hbm, hb...  141 us
    slice x1, local copies, waits for them, and re-layouts, shards(): return padded[:, :, EDGE - SC:EDGE - SC + cols]  3.45 us

profile of v1, /device:TPU:0, one launch (start us, length us, event | category | flops | bytes accessed | tf_op | source)
XLA Modules:
  0.0 144.6 jit_solution(15524833372479936033)
XLA Ops:
  0.0 141.1 %whole.1 = bf16[3,6,104,512]{3,2,1,0:T(8,128)(2,1)} custom-call(bf16[3,6,384,512]{3,2,1,0:T(8,128)(2,1)} %levels_hbm.1, f32[1,512]{1,0:T(1,128)} %bitcast.3, f32[3,512]{1,0:T(4,128)} %embed.1, f32[3,512]{1,0:T(4,128)} %lq.1, bf16[512,512]{1,0:T(8,128)(2,1)} %q_hbm.1, bf16[512,512]{1,0:T(8,128)(2,1)} %k_hbm.1, bf16[512,512]{1,0:T(8,128)(2,1)} %v_hbm.1, ...), custom_call_target="tpu_custom_call" | custom-call | tf_op jit(solution)/shard_map/whole/pallas_call | solution.py:552
  141.1 3.5 %slice.3 = bf16[3,6,96,512]{3,2,1,0:T(8,128)(2,1)} slice(bf16[3,6,104,512]{3,2,1,0:T(8,128)(2,1)} %whole.1), slice={[0:3], [0:6], [2:98], [0:512]} | slice | bytes 3538944 | tf_op jit(solution)/shard_map/slice | solution.py:618

commit v2 on v1

--- a/solution.py
+++ b/solution.py
@@ -14,7 +14,7 @@
 LANES = 128
 STEP = 2 * WC
 EDGE = 8
-LEAD = 2
+LEAD = 3
 BF = jnp.bfloat16
 F32 = jnp.float32
 MESH = pl.DeviceIdType.MESH
@@ -68,9 +68,7 @@
     xb,
     mine,
     arrived,
-    head,
-    tail,
-    ahead,
+    latent_rows,
     own,
     back,
     q_mat,
@@ -80,13 +78,17 @@
     ones_t,
     padded,
     mask,
+    middle,
+    both,
+    query,
+    perm,
+    perm_t,
     w_sem,
     xa_sem,
     xb_sem,
+    x_send,
     z_send,
     z_recv,
-    head_send,
-    head_recv,
     own_sem,
     back_send,
     back_recv,
@@ -108,6 +110,7 @@
     side = latents * tokens
     raw_rows = levels * tokens
     lead = LEAD
+    win_rows = mask.shape[0]
     is_end = (me == 0) | (me == n - 1)
 
     up_level = lax.rem(me + 1, n)
@@ -116,15 +119,23 @@
     down_space = lax.rem(place + spaces - 1, spaces)
 
     barrier = pltpu.get_barrier_semaphore()
-    for target in (
-        {"level": up_level},
-        {"level": down_level},
-        {"space": up_space},
-        {"space": down_space},
-        {"space": up_space, "level": up_level},
-        {"space": down_space, "level": down_level},
-    ):
+    for target in ({"space": up_space}, {"space": down_space}):
         pl.semaphore_signal(barrier, inc=1, device_id=target, device_id_type=MESH)
+
+    @pl.when(me < n - 1)
+    def _():
+        pl.semaphore_signal(
+            barrier, inc=1, device_id={"level": up_level}, device_id_type=MESH
+        )
+
+    @pl.when(me > 0)
+    def _():
+        pl.semaphore_signal(
+            barrier, inc=1, device_id={"level": down_level}, device_id_type=MESH
+        )
+
+    def enter():
+        pl.semaphore_wait(barrier, jnp.where(is_end, 3, 4))
 
     def dest_of(j):
         return jnp.where(2 * me < n, n - 1 - j, j)
@@ -149,22 +160,49 @@
         )
         return [pltpu.make_async_copy(a, b, w_sem.at[i]) for i, (a, b) in enumerate(pairs)]
 
+    def chunk_and_side(u):
+        order = u + jnp.where(u == 1, 1, jnp.where(u == 2, -1, 0))
+        return lax.div(order, 2), lax.rem(order, 2)
+
+    def x_spans(d, i):
+        start = pl.multiple_of(d * cols + chunk_of(i) * STEP, EDGE)
+        rest = pl.multiple_of(lax.rem(start + STEP, all_cols), EDGE)
+        return pl.ds(start, STEP), pl.ds(rest, EDGE)
+
     def x_copies(d, u):
-        band = pl.ds(lax.rem(u, 2) * SR, SR)
-        start = pl.multiple_of(d * cols + chunk_of(lax.div(u, 2)) * STEP, EDGE)
-        rest = pl.multiple_of(lax.rem(start + STEP, all_cols), EDGE)
+        main, more = x_spans(d, chunk_and_side(u)[0])
+        band = pl.ds(SR, SR)
         return (
-            pltpu.make_async_copy(
-                levels_hbm.at[:, band, pl.ds(start, STEP)], xa.at[d, u], xa_sem.at[d, u]
+            pltpu.make_async_copy(levels_hbm.at[:, band, main], xa.at[d, u], xa_sem.at[d, u]),
+            pltpu.make_async_copy(levels_hbm.at[:, band, more], xb.at[d, u], xb_sem.at[d, u]),
+        )
+
+    def x_sends(d, u):
+        main, more = x_spans(d, chunk_and_side(u)[0])
+        band = pl.ds(0, SR)
+        return (
+            pltpu.make_async_remote_copy(
+                src_ref=levels_hbm.at[:, band, main],
+                dst_ref=xa.at[d, u],
+                send_sem=x_send.at[0],
+                recv_sem=xa_sem.at[d, u],
+                device_id={"space": down_space},
+                device_id_type=MESH,
             ),
-            pltpu.make_async_copy(
-                levels_hbm.at[:, band, pl.ds(rest, EDGE)], xb.at[d, u], xb_sem.at[d, u]
+            pltpu.make_async_remote_copy(
+                src_ref=levels_hbm.at[:, band, more],
+                dst_ref=xb.at[d, u],
+                send_sem=x_send.at[1],
+                recv_sem=xb_sem.at[d, u],
+                device_id={"space": down_space},
+                device_id_type=MESH,
             ),
         )
 
     def each_unit(first, last, act):
         def body(k, carry):
-            d = dest_of(lax.rem(k, n))
+            j = lax.rem(k, n)
+            d = dest_of(jnp.where(j == 0, 0, jnp.where(j == 1, n - 2, jnp.where(j == n - 1, j, j - 1))))
             u = lax.div(k, n) - lead + lead_of(d)
 
             @pl.when((u >= 0) & (u < units))
@@ -176,30 +214,28 @@
         lax.fori_loop(first, last, body, 0)
 
     def start_x(d, u):
-        for copy in x_copies(d, u):
-            copy.start()
+        @pl.when(chunk_and_side(u)[1] == 0)
+        def _():
+            for copy in x_copies(d, u):
+                copy.start()
+
+    def push_x(d, u):
+        @pl.when(chunk_and_side(u)[1] == 1)
+        def _():
+            for copy in x_sends(d, u):
+                copy.start()
 
     def send(d, u, right, count):
         return pltpu.make_async_remote_copy(
             src_ref=mine.at[d, u, pl.ds(0, count)],
             dst_ref=arrived.at[0 if right else 1, d, u, pl.ds(0, count)],
-            send_sem=z_send.at[d, u],
+            send_sem=z_send.at[0],
             recv_sem=z_recv.at[0 if right else 1, d, u],
             device_id={"level": up_level if right else down_level},
             device_id_type=MESH,
         )
 
     sum_rows = mine.shape[2]
-
-    def send_head(i):
-        return pltpu.make_async_remote_copy(
-            src_ref=head.at[i],
-            dst_ref=ahead.at[i],
-            send_sem=head_send.at[i],
-            recv_sem=head_recv.at[i],
-            device_id={"space": down_space},
-            device_id_type=MESH,
-        )
 
     def column_of(i):
         return pl.multiple_of(EDGE + chunk_of(i) * STEP, EDGE)
@@ -243,8 +279,16 @@
         )
 
     def level_tokens(d, u):
-        for copy in x_copies(d, u):
-            copy.wait()
+        @pl.when(chunk_and_side(u)[1] == 0)
+        def _():
+            for copy in x_copies(d, u):
+                copy.wait()
+
+        @pl.when(chunk_and_side(u)[1] == 1)
+        def _():
+            for copy in x_sends(d, u):
+                copy.wait_recv()
+
         normed = []
         for l in range(levels):
             x = jnp.concatenate([xa[d, u, l].astype(F32), xb[d, u, l].astype(F32)], 1)
@@ -258,12 +302,15 @@
     each_unit(0, early, start_x)
     for copy in weights[:3]:
         copy.start()
-    pl.semaphore_wait(barrier, 6)
 
     def send_tokens(d, u):
         @pl.when(d != me)
         def _():
             mine[d, u, :raw_rows, :] = level_tokens(d, u).astype(BF)
+
+            @pl.when((d == dest_of(0)) & (u == 0))
+            def _():
+                enter()
 
             @pl.when(me == 0)
             def _():
@@ -275,15 +322,20 @@
 
     @pl.when(is_end)
     def _():
-        each_unit(0, early, send_tokens)
-
+        each_unit(0, 1, send_tokens)
+
+    @pl.when(jnp.logical_not(is_end))
+    def _():
+        enter()
+
+    each_unit(0, total_steps, push_x)
     each_unit(early, total_steps, start_x)
     for copy in weights[3:]:
         copy.start()
 
     @pl.when(is_end)
     def _():
-        each_unit(early, total_steps, send_tokens)
+        each_unit(1, total_steps, send_tokens)
 
     ones[...] = (
         (iota((width, LANES), 0) // head_dim == lax.rem(iota((width, LANES), 1), heads))
@@ -351,6 +403,8 @@
         tokens_left = left & (me == 1)
         tokens_right = right & (me == n - 2)
 
+        both[:raw_rows, :] = level_tokens(d, u)
+
         @pl.when(tokens_left)
         def _():
             send(d, u, True, raw_rows).wait_recv()
@@ -362,13 +416,12 @@
         @pl.when(tokens_left | tokens_right)
         def _():
             which = jnp.where(me == 1, 0, 1)
-            more = arrived[which, d, u, :raw_rows, :].astype(F32)
-            both = jnp.concatenate([level_tokens(d, u), more], 0).astype(BF)
-            mine[d, u] = partial(both).astype(BF)
+            both[raw_rows:, :] = arrived[which, d, u, :raw_rows, :].astype(F32)
+            mine[d, u] = partial(both[...].astype(BF)).astype(BF)
 
         @pl.when(jnp.logical_not(tokens_left | tokens_right))
         def _():
-            mine[d, u] = partial(level_tokens(d, u).astype(BF)).astype(BF)
+            mine[d, u] = partial(both[:raw_rows, :].astype(BF)).astype(BF)
 
         @pl.when(left & (me > 1))
         def _():
@@ -392,36 +445,47 @@
         total = mine[me, u].astype(F32)
         turned = jnp.concatenate([total[side:], jnp.zeros((8, width), F32)], 0).T.astype(BF)
         pooled = []
-        query = []
         for a in range(latents):
             denom = dot(turned[a * LANES : (a + 1) * LANES], den_spread[...])[:tokens]
             pooled.append(total[a * tokens : (a + 1) * tokens] / denom)
-            query.append(jnp.broadcast_to(lq[a : a + 1, :], (tokens, width)))
         pooled = jnp.concatenate(pooled, 0).astype(BF)
-        value = (jnp.concatenate(query, 0) + dot(pooled, out_w[...])).astype(BF)
-        i = lax.div(u, 2)
-
-        @pl.when(lax.rem(u, 2) == 0)
-        def _():
-            head[i] = value
-            send_head(i).start()
-
-        @pl.when(lax.rem(u, 2) == 1)
-        def _():
-            tail[...] = value
+        pooled = dot(perm[...], pooled).astype(BF)
+        i, which = chunk_and_side(u)
+        latent_rows[lax.rem(i, 2), which] = (query[...] + dot(pooled, out_w[...])).astype(BF)
 
     scale_row = jnp.zeros((1, LANES), F32)
     for h in range(heads):
         scale_row = jnp.where(iota((1, LANES), 1) == h, swin[h] / head_dim, scale_row)
-    row = iota((2 * side, 2 * side), 0)
-    col = iota((2 * side, 2 * side), 1)
-    window = lax.rem(row, STEP) // WC == lax.rem(col, STEP) // WC
-    region = (row >= side) == (col >= side)
-    mask[...] = jnp.where(window & (region | (place < spaces - 1)), 1.0, 0.0)
-
-    def layer(i):
-        send_head(i).wait_recv()
-        block = jnp.concatenate([tail[...].astype(F32), ahead[i].astype(F32)], 0)
+    part = win_rows // 2
+    row = iota((win_rows, win_rows), 0)
+    col = iota((win_rows, win_rows), 1)
+    region = (row >= part) == (col >= part)
+    valid = lax.rem(col, part) < side // 2
+    mask[...] = jnp.where(valid & (region | (place < spaces - 1)), 1.0, 0.0)
+
+    def place_of(spot):
+        inner = lax.rem(spot, part)
+        grid = lax.div(inner, WC) * STEP + lax.div(spot, part) * WC + lax.rem(inner, WC)
+        return jnp.where(inner < side // 2, grid, -1)
+
+    size = (win_rows, side)
+    perm[...] = (place_of(iota(size, 0)) == iota(size, 1)).astype(F32).astype(BF)
+    size = (side, win_rows)
+    perm_t[...] = (place_of(iota(size, 1)) == iota(size, 0)).astype(F32).astype(BF)
+    owner = lax.div(lax.rem(iota((win_rows, width), 0), part), SR * WC)
+    rows_of = jnp.broadcast_to(lq[0:1, :], (win_rows, width))
+    for a in range(1, latents):
+        rows_of = jnp.where(owner == a, lq[a : a + 1, :], rows_of)
+    query[...] = rows_of
+
+    def attention(i):
+        slot = lax.rem(i, 2)
+        pieces = [
+            latent_rows[slot, which, w * part : (w + 1) * part, :]
+            for w in range(2)
+            for which in range(2)
+        ]
+        block = jnp.concatenate(pieces, 0).astype(F32)
         normed = layer_norm(block, attn_gain[...]).astype(BF)
         packed = dot(normed, qkv_w[...]).astype(BF)
         q = packed[:, :width]
@@ -433,27 +497,40 @@
         q_norm = lax.rsqrt(q_norm * (1.0 / head_dim) + 1e-06) * scale_row
         k_norm = dot_t(ones_t[...], (k32 * k32).astype(BF))
         k_norm = lax.rsqrt(k_norm * (1.0 / head_dim) + 1e-06)
-        mixed = []
-        for h in range(heads):
-            cut = slice(h * head_dim, (h + 1) * head_dim)
-            scores = dot_t(q[:, cut], k[:, cut])
-            scores = scores * q_norm[:, h : h + 1] * k_norm[h : h + 1, :]
-            weights = jnp.exp(scores) * mask[...]
-            norm = jnp.sum(weights, -1, keepdims=True)
-            mixed.append(dot(weights.astype(BF), v[:, cut]) / norm)
-        mixed = jnp.concatenate(mixed, 1).astype(BF)
+        windows = []
+        for w in range(2):
+            here = slice(w * win_rows, (w + 1) * win_rows)
+            mixed = []
+            for h in range(heads):
+                cut = slice(h * head_dim, (h + 1) * head_dim)
+                scores = dot_t(q[here, cut], k[here, cut])
+                scores = scores * q_norm[here, h : h + 1] * k_norm[h : h + 1, here]
+                weights = jnp.exp(scores) * mask[...]
+                norm = jnp.sum(weights, -1, keepdims=True)
+                mixed.append(dot(weights.astype(BF), v[here, cut]) / norm)
+            windows.append(jnp.concatenate(mixed, 1))
+        mixed = jnp.concatenate(windows, 0).astype(BF)
         branch = dot(mixed, proj_w[...]).astype(BF)
-        middle = block + branch.astype(F32)
-
-        def feed(part):
-            mlp_in = layer_norm(part, mlp_gain[...]).astype(BF)
-            hidden = jax.nn.gelu(dot(mlp_in, up_w[...])).astype(BF)
-            final = part + dot(hidden, down_w[...])
-            return final.reshape(latents, SR, STEP, width).astype(BF)
-
-        back[i] = feed(middle[side:])
+        middle[slot] = block + branch.astype(F32)
+
+    def feed(i, which):
+        slot = lax.rem(i, 2)
+        pieces = []
+        for w in range(2):
+            start = w * win_rows + which * part
+            pieces.append(middle[slot, start : start + part, :])
+        rows_in = jnp.concatenate(pieces, 0)
+        mlp_in = layer_norm(rows_in, mlp_gain[...]).astype(BF)
+        hidden = jax.nn.gelu(dot(mlp_in, up_w[...])).astype(BF)
+        final = (rows_in + dot(hidden, down_w[...])).astype(BF)
+        return dot(perm_t[...], final).reshape(latents, SR, STEP, width).astype(BF)
+
+    def feed_back(i):
+        back[i] = feed(i, 1)
         send_back(i).start()
-        own[i] = feed(middle[:side])
+
+    def feed_own(i):
+        own[i] = feed(i, 0)
         keep_own(i).start()
 
         @pl.when(i == 0)
@@ -461,54 +538,89 @@
             for copy in edge_copies():
                 copy.start()
 
+    def finish_unit(u):
+        @pl.when(u == 0)
+        def _():
+            for copy in weights[3:]:
+                copy.wait()
+
+        @pl.when((u >= 0) & (u < units))
+        def _():
+            latent(u)
+
+        even = lax.rem(u, 2) == 0
+
+        @pl.when((u == 3) | ((u >= 4) & even))
+        def _():
+            feed_back(jnp.where(u == 3, 0, lax.div(u, 2) - 1))
+
+        def feeds_own(k, c):
+            feed_own(jnp.where(u == 3, 0, lax.div(u, 2) - 1 - k))
+            return c
+
+        one = (u == 3) | (even & (u >= 4) & (u != units - 2))
+        count = jnp.where(u == units, 2, jnp.where(one, 1, 0))
+        lax.fori_loop(0, count, feeds_own, 0)
+
+        chunk, which = chunk_and_side(u)
+
+        @pl.when((u >= 2) & (u < units) & (which == 1))
+        def _():
+            attention(chunk)
+
     def step(v, carry):
         def body(k, c):
-            d = dest_of(jnp.where(k == 0, 0, jnp.where(k == 1, n - 1, k - 1)))
+            mine_at = jnp.where(2 * me < n, n - 1 - me, me)
+            other = dest_of(jnp.where(k - 1 < mine_at, k - 1, k))
+            d = jnp.where(k == 0, dest_of(0), jnp.where(k == 1, me, other))
             u = v - lead + lead_of(d)
 
             @pl.when((u >= 0) & (u < units) & ((d == me) | jnp.logical_not(is_end)))
             def _():
                 collect(d, u)
 
+            @pl.when(k == 1)
+            def _():
+                finish_unit(u)
+
             return c
 
         lax.fori_loop(0, n, body, 0)
-
-        @pl.when(v == lead)
-        def _():
-            for copy in weights[3:]:
-                copy.wait()
-
-        @pl.when(v >= lead)
-        def _():
-            latent(v - lead)
-
-            @pl.when(lax.rem(v - lead, 2) == 1)
-            def _():
-                layer(lax.div(v - lead, 2))
-
         return carry
 
-    lax.fori_loop(0, units + lead, step, 0)
-
-    def drain(d, u):
-        @pl.when((d != me) & is_end)
-        def _():
-            send(d, u, True, raw_rows).wait_send()
-
-        @pl.when((d != me) & jnp.logical_not(is_end))
-        def _():
-            send(d, u, True, sum_rows).wait_send()
-
-    each_unit(0, total_steps, drain)
-
-    def finish(i, carry):
-        send_head(i).wait_send()
+    lax.fori_loop(0, units + lead + 1, step, 0)
+
+    def sent(count):
+        return pltpu.make_async_remote_copy(
+            src_ref=mine.at[pl.ds(0, n - 1), :, pl.ds(0, count)],
+            dst_ref=arrived.at[0, pl.ds(0, n - 1), :, pl.ds(0, count)],
+            send_sem=z_send.at[0],
+            recv_sem=z_recv.at[0, 0, 0],
+            device_id={"level": up_level},
+            device_id_type=MESH,
+        )
+
+    @pl.when(is_end)
+    def _():
+        sent(raw_rows).wait_send()
+
+    @pl.when(jnp.logical_not(is_end))
+    def _():
+        sent(sum_rows).wait_send()
+
+    for which, (buffer, sem) in enumerate(((xa, xa_sem), (xb, xb_sem))):
+        pushed = buffer.at[:, pl.ds(0, chunks)]
+        pltpu.make_async_remote_copy(
+            src_ref=pushed,
+            dst_ref=pushed,
+            send_sem=x_send.at[which],
+            recv_sem=sem.at[0, 0],
+            device_id={"space": down_space},
+            device_id_type=MESH,
+        ).wait_send()
+    for i in range(chunks):
         keep_own(i).wait()
         send_back(i).wait()
-        return carry
-
-    lax.fori_loop(0, chunks, finish, 0)
     for copy in edge_copies():
         copy.wait()
 
@@ -542,8 +654,9 @@
     tokens = SR * STEP
     side = latents * tokens
     sum_rows = side + 8
+    win_rows = 2 * (-(-side // 32) * 16)
     assert rows == WR and heads == 8 and tokens <= LANES and latents * heads <= LANES
-    assert cols % STEP == 0 and n >= 4 and levels * tokens <= sum_rows
+    assert cols % STEP == 0 and n >= 4 and chunks >= 4 and levels * tokens <= sum_rows
 
     hbm = pl.BlockSpec(memory_space=pl.ANY)
     vmem = pl.BlockSpec(memory_space=pltpu.VMEM)
@@ -568,9 +681,7 @@
             pltpu.VMEM((n, units, levels, SR, EDGE, width), BF),
             pltpu.VMEM((n, units, sum_rows, width), BF),
             pltpu.VMEM((2, n, units, sum_rows, width), BF),
-            pltpu.VMEM((chunks, side, width), BF),
-            pltpu.VMEM((side, width), BF),
-            pltpu.VMEM((chunks, side, width), BF),
+            pltpu.VMEM((2, 2, win_rows, width), BF),
             pltpu.VMEM((chunks, latents, SR, STEP, width), BF),
             pltpu.VMEM((chunks, latents, SR, STEP, width), BF),
             pltpu.VMEM((2 * LANES, width), BF),
@@ -579,14 +690,18 @@
             pltpu.VMEM((16, width), BF),
             pltpu.VMEM((16, width), BF),
             pltpu.VMEM((16, width), F32),
-            pltpu.VMEM((2 * side, 2 * side), F32),
+            pltpu.VMEM((win_rows, win_rows), F32),
+            pltpu.VMEM((2, 2 * win_rows, width), F32),
+            pltpu.VMEM((2 * levels * tokens, width), F32),
+            pltpu.VMEM((win_rows, width), F32),
+            pltpu.VMEM((win_rows, side), BF),
+            pltpu.VMEM((side, win_rows), BF),
             sem((8,)),
             sem((n, units)),
             sem((n, units)),
-            sem((n, units)),
+            sem((2,)),
+            sem((1,)),
             sem((2, n, units)),
-            sem((chunks,)),
-            sem((chunks,)),
             sem((chunks,)),
             sem((chunks,)),
             sem((chunks,)),

time: 145 us -> 137 us (0.945)
  Pallas kernels: 141 us -> 132 us
    pallas_call x1, Pallas kernels: 141 us -> 132 us  [shards(): pl.pallas_call(kernel, in_specs=[hbm, vmem, vmem, vmem, hbm, hbm, hbm, hb...]
where the time goes in v2:
time: 137 us; the launch traced here: 136 us
  Pallas kernels  132 us (96%)
  local copies, waits for them, and re-layouts  3.45 us (3%)
    pallas_call x1, Pallas kernels, shards(): pl.pallas_call(kernel, in_specs=[hbm, vmem, vmem, vmem, hbm, hbm, hbm, hb...  132 us
    slice x1, local copies, waits for them, and re-layouts, shards(): return padded[:, :, EDGE - SC:EDGE - SC + cols]  3.45 us

profile of v2, /device:TPU:0, one launch (start us, length us, event | category | flops | bytes accessed | tf_op | source)
XLA Modules:
  0.0 136.0 jit_solution(11966988053066128135)
XLA Ops:
  0.0 132.5 %whole.1 = bf16[3,6,104,512]{3,2,1,0:T(8,128)(2,1)} custom-call(bf16[3,6,384,512]{3,2,1,0:T(8,128)(2,1)} %levels_hbm.1, f32[1,512]{1,0:T(1,128)} %bitcast.3, f32[3,512]{1,0:T(4,128)} %embed.1, f32[3,512]{1,0:T(4,128)} %lq.1, bf16[512,512]{1,0:T(8,128)(2,1)} %q_hbm.1, bf16[512,512]{1,0:T(8,128)(2,1)} %k_hbm.1, bf16[512,512]{1,0:T(8,128)(2,1)} %v_hbm.1, ...), custom_call_target="tpu_custom_call" | custom-call | tf_op jit(solution)/shard_map/whole/pallas_call | solution.py:665
  132.5 3.5 %slice.3 = bf16[3,6,96,512]{3,2,1,0:T(8,128)(2,1)} slice(bf16[3,6,104,512]{3,2,1,0:T(8,128)(2,1)} %whole.1), slice={[0:3], [0:6], [2:98], [0:512]} | slice | bytes 3538944 | tf_op jit(solution)/shard_map/slice | solution.py:733

commit v3 on v2

--- a/solution.py
+++ b/solution.py
@@ -625,6 +625,20 @@
         copy.wait()
 
 
+def shift_kernel(padded, out_hbm, ready, sems):
+    latents, rows, cols, _ = ready.shape
+    copies = []
+    for a in range(latents):
+        for r in range(rows):
+            row = padded[a, r].astype(F32)
+            ready[a, r] = row[EDGE - SC : EDGE - SC + cols].astype(BF)
+        copy = pltpu.make_async_copy(ready.at[a], out_hbm.at[a], sems.at[a])
+        copy.start()
+        copies.append(copy)
+    for copy in copies:
+        copy.wait()
+
+
 def shards(
     levels_in,
     kv_gain,
@@ -666,8 +680,8 @@
         kernel,
         in_specs=[hbm, vmem, vmem, vmem, hbm, hbm, hbm, hbm, smem, vmem, hbm, smem, hbm, vmem]
         + [hbm, hbm],
-        out_specs=hbm,
-        out_shape=jax.ShapeDtypeStruct((latents, rows, cols + EDGE, width), BF),
+        out_specs=vmem,
+        out_shape=pltpu.VMEM((latents, rows, cols + EDGE, width), BF),
         scratch_shapes=[
             pltpu.VMEM((width, width), BF),
             pltpu.VMEM((width, width), BF),
@@ -709,7 +723,7 @@
             sem((2,)),
         ],
         compiler_params=pltpu.CompilerParams(
-            collective_id=0, has_side_effects=True, vmem_limit_bytes=63 * 1024 * 1024
+            collective_id=0, has_side_effects=True, vmem_limit_bytes=59 * 1024 * 1024
         ),
         name="whole",
     )(
@@ -730,7 +744,15 @@
         up_weight,
         down_weight,
     )
-    return padded[:, :, EDGE - SC : EDGE - SC + cols]
+    return pl.pallas_call(
+        shift_kernel,
+        in_specs=[vmem],
+        out_specs=hbm,
+        out_shape=jax.ShapeDtypeStruct((latents, rows, cols, width), BF),
+        scratch_shapes=[pltpu.VMEM((latents, rows, cols, width), BF), sem((latents,))],
+        compiler_params=pltpu.CompilerParams(vmem_limit_bytes=16 * 1024 * 1024),
+        name="shift",
+    )(padded)
 
 
 def solution(mesh):

time: 137 us -> 134 us (0.978)
  local copies, waits for them, and re-layouts: 3.45 us -> 0 us
    slice x1 -> x0, local copies, waits for them, and re-layouts: 3.45 us -> none  [shards(): return padded[:, :, EDGE - SC:EDGE - SC + cols]]
where the time goes in v3:
time: 134 us; the launch traced here: 133 us
  Pallas kernels  133 us (99%)
    pallas_call x1, Pallas kernels, shards(): pl.pallas_call(kernel, in_specs=[hbm, vmem, vmem, vmem, hbm, hbm, hbm, hb...  132 us

profile of v3, /device:TPU:0, one launch (start us, length us, event | category | flops | bytes accessed | tf_op | source)
XLA Modules:
  0.0 133.3 jit_solution(14435963441007051987)
XLA Ops:
  0.0 132.0 %whole.1.padded = bf16[3,6,104,512]{3,2,1,0:T(8,128)(2,1)S(1)} custom-call(bf16[3,6,384,512]{3,2,1,0:T(8,128)(2,1)} %levels_hbm.1, f32[1,512]{1,0:T(1,128)} %bitcast.3, f32[3,512]{1,0:T(4,128)} %embed.1, f32[3,512]{1,0:T(4,128)} %lq.1, bf16[512,512]{1,0:T(8,128)(2,1)} %q_hbm.1, bf16[512,512]{1,0:T(8,128)(2,1)} %k_hbm.1, bf16[512,512]{1,0:T(8,128)(2,1)} %v_hbm.1, ...), custom_call_target="tpu_custom_call" | custom-call | tf_op jit(solution)/shard_map/whole/pallas_call | solution.py:679
  132.0 1.3 shift.1

commit v4 on v3

--- a/solution.py
+++ b/solution.py
@@ -53,9 +53,9 @@
     swin,
     proj_hbm,
     mlp_gain,
-    up_hbm,
+    upadded_out,
     down_hbm,
-    p_hbm,
+    padded_out,
     q_w,
     k_w,
     v_w,
@@ -89,7 +89,6 @@
     x_send,
     z_send,
     z_recv,
-    own_sem,
     back_send,
     back_recv,
     edge_send,
@@ -119,8 +118,7 @@
     down_space = lax.rem(place + spaces - 1, spaces)
 
     barrier = pltpu.get_barrier_semaphore()
-    for target in ({"space": up_space}, {"space": down_space}):
-        pl.semaphore_signal(barrier, inc=1, device_id=target, device_id_type=MESH)
+    pl.semaphore_signal(barrier, inc=1, device_id={"space": up_space}, device_id_type=MESH)
 
     @pl.when(me < n - 1)
     def _():
@@ -135,7 +133,7 @@
         )
 
     def enter():
-        pl.semaphore_wait(barrier, jnp.where(is_end, 3, 4))
+        pl.semaphore_wait(barrier, jnp.where(is_end, 2, 3))
 
     def dest_of(j):
         return jnp.where(2 * me < n, n - 1 - j, j)
@@ -155,7 +153,7 @@
             (out_hbm, out_w),
             (qkv_hbm, qkv_w),
             (proj_hbm, proj_w),
-            (up_hbm, up_w),
+            (upadded_out, up_w),
             (down_hbm, down_w),
         )
         return [pltpu.make_async_copy(a, b, w_sem.at[i]) for i, (a, b) in enumerate(pairs)]
@@ -243,26 +241,19 @@
     def send_back(i):
         return pltpu.make_async_remote_copy(
             src_ref=back.at[i],
-            dst_ref=p_hbm.at[:, pl.ds(0, SR), pl.ds(column_of(i), STEP)],
+            dst_ref=padded_out.at[:, pl.ds(0, SR), pl.ds(column_of(i), STEP)],
             send_sem=back_send.at[i],
             recv_sem=back_recv.at[i],
             device_id={"space": up_space},
             device_id_type=MESH,
         )
 
-    def keep_own(i):
-        return pltpu.make_async_copy(
-            own.at[i],
-            p_hbm.at[:, pl.ds(SR, SR), pl.ds(column_of(i), STEP)],
-            own_sem.at[i],
-        )
-
     def edge_copies():
         cut = pl.ds(STEP - EDGE, EDGE)
         return (
             pltpu.make_async_remote_copy(
-                src_ref=own.at[0, :, :, cut],
-                dst_ref=p_hbm.at[:, pl.ds(SR, SR), pl.ds(0, EDGE)],
+                src_ref=own,
+                dst_ref=padded_out.at[:, pl.ds(SR, SR), pl.ds(0, EDGE)],
                 send_sem=edge_send.at[0],
                 recv_sem=edge_recv.at[0],
                 device_id={"level": up_level},
@@ -270,7 +261,7 @@
             ),
             pltpu.make_async_remote_copy(
                 src_ref=back.at[0, :, :, cut],
-                dst_ref=p_hbm.at[:, pl.ds(0, SR), pl.ds(0, EDGE)],
+                dst_ref=padded_out.at[:, pl.ds(0, SR), pl.ds(0, EDGE)],
                 send_sem=edge_send.at[1],
                 recv_sem=edge_recv.at[1],
                 device_id={"space": up_space, "level": up_level},
@@ -297,11 +288,8 @@
         return jnp.concatenate(normed, 0)
 
     total_steps = (units + lead) * n
-    early = (lead + 1) * n
     weights = weight_copies()
-    each_unit(0, early, start_x)
-    for copy in weights[:3]:
-        copy.start()
+    start_x(dest_of(0), 0)
 
     def send_tokens(d, u):
         @pl.when(d != me)
@@ -328,9 +316,9 @@
     def _():
         enter()
 
-    each_unit(0, total_steps, push_x)
-    each_unit(early, total_steps, start_x)
-    for copy in weights[3:]:
+    each_unit(1, total_steps, start_x)
+    each_unit(1, total_steps, push_x)
+    for copy in weights:
         copy.start()
 
     @pl.when(is_end)
@@ -530,11 +518,12 @@
         send_back(i).start()
 
     def feed_own(i):
-        own[i] = feed(i, 0)
-        keep_own(i).start()
+        value = feed(i, 0)
+        padded_out[:, SR:, pl.ds(column_of(i), STEP), :] = value
 
         @pl.when(i == 0)
         def _():
+            own[...] = value[:, :, STEP - EDGE :]
             for copy in edge_copies():
                 copy.start()
 
@@ -619,7 +608,6 @@
             device_id_type=MESH,
         ).wait_send()
     for i in range(chunks):
-        keep_own(i).wait()
         send_back(i).wait()
     for copy in edge_copies():
         copy.wait()
@@ -696,7 +684,7 @@
             pltpu.VMEM((n, units, sum_rows, width), BF),
             pltpu.VMEM((2, n, units, sum_rows, width), BF),
             pltpu.VMEM((2, 2, win_rows, width), BF),
-            pltpu.VMEM((chunks, latents, SR, STEP, width), BF),
+            pltpu.VMEM((latents, SR, EDGE, width), BF),
             pltpu.VMEM((chunks, latents, SR, STEP, width), BF),
             pltpu.VMEM((2 * LANES, width), BF),
             pltpu.VMEM((width, LANES), BF),
@@ -716,7 +704,6 @@
             sem((2,)),
             sem((1,)),
             sem((2, n, units)),
-            sem((chunks,)),
             sem((chunks,)),
             sem((chunks,)),
             sem((2,)),

time: 134 us -> 134 us (level)
  no operation moved by 1% of the time
where the time goes in v4:
time: 134 us; the launch traced here: 133 us
  Pallas kernels  133 us (99%)
    pallas_call x1, Pallas kernels, shards(): pl.pallas_call(kernel, in_specs=[hbm, vmem, vmem, vmem, hbm, hbm, hbm, hb...  132 us

profile of v4, /device:TPU:0, one launch (start us, length us, event | category | flops | bytes accessed | tf_op | source)
XLA Modules:
  0.0 133.2 jit_solution(2977635974326493866)
XLA Ops:
  0.0 131.9 %whole.1.padded = bf16[3,6,104,512]{3,2,1,0:T(8,128)(2,1)S(1)} custom-call(bf16[3,6,384,512]{3,2,1,0:T(8,128)(2,1)} %levels_hbm.1, f32[1,512]{1,0:T(1,128)} %bitcast.3, f32[3,512]{1,0:T(4,128)} %embed.1, f32[3,512]{1,0:T(4,128)} %lq.1, bf16[512,512]{1,0:T(8,128)(2,1)} %q_hbm.1, bf16[512,512]{1,0:T(8,128)(2,1)} %k_hbm.1, bf16[512,512]{1,0:T(8,128)(2,1)} %v_hbm.1, ...), custom_call_target="tpu_custom_call" | custom-call | tf_op jit(solution)/shard_map/whole/pallas_call | solution.py:667
  131.9 1.3 shift.1
